TPU v7x, 256 devices: a whole 4x4x8 slice. The times are simulated.
256 devices in a mesh: seq: 16 (over y, z_lo), expert: 8 (over x, core), batch: 2 (over z_hi).
Axes of the slice: x: 4, y: 4, z: 8 (z_hi: 2, z_lo: 4; z = z_hi * 4 + z_lo), core: 2. Of those that a mesh axis runs over, the one named last changes fastest.
Arguments:
- hidden_state: bfloat16 [64, 4096], P(('batch', 'expert'), 'seq'), may hold values from -9 to 9
- queries: bfloat16 [64, 2048], P(('batch', 'expert'), 'seq'), may hold values from -180 to 180
- page_table: int32 [64, 16, 4], P(('batch', 'expert'), 'seq'), may hold values from 0 to 19, as said below
- lengths: int32 [64], P(('batch', 'expert')), may hold values from 2048 to 8192
- paged_keys: bfloat16 [16, 320, 128, 512], P(('batch', 'expert'), 'seq'), may hold values from -6 to 6
- paged_values: bfloat16 [16, 320, 128, 512], P(('batch', 'expert'), 'seq'), may hold values from -6 to 6
- out_weight: bfloat16 [2048, 4096], P('seq', 'expert'), may hold values from -1.5 to 1.5
- norm_gain: float32 [4096], P('seq'), may hold values from 0.25 to 1.75
- expert_ids: int32 [64, 2], P(('batch', 'expert')), may hold values from 0 to 7, all different within a row; in each aligned block of 4 rows (0 to 3, 4 to 7, ...) at most 2 rows name the same one
- route_weights: float32 [64, 2], P(('batch', 'expert')), may hold values from 0.25 to 1
- expert_gate: bfloat16 [8, 4096, 8192], P('expert', None, ('seq', 'batch')), may hold values from -0.09375 to 0.09375
- expert_up: bfloat16 [8, 4096, 8192], P('expert', None, ('seq', 'batch')), may hold values from -0.09375 to 0.09375
- expert_down: bfloat16 [8, 8192, 4096], P('expert', ('seq', 'batch')), may hold values from -0.0625 to 0.0625
Outputs:
- layer_out: bfloat16 [64, 4096], P(('batch', 'expert'), 'seq')
Inputs may be any that keep to these rules, and one draw needn't show every extreme that they name: `page_table`: the page ids of one block's sequences on one shard are all different. `expert_ids`: a token's two experts differ; within the 4 rows of one device no expert is named more than 2 times.
All inputs are finite; a program needn't handle non-finite values.
Results may differ from a plain program's by a relative error of at most 0.006.
Values may be sent and summed in bfloat16 or wider, within the bound.
A program may use at most 64 MiB of HBM per device.

v0:
```python
import math

import jax
import jax.numpy as jnp
from jax import lax
from jax.sharding import PartitionSpec as P

D = 4096
QUERY_HEADS = 16
KEY_VALUE_HEADS = 4
HEAD_DIM = 128
PAGE_TOKENS = 128
SEQUENCE_SLOTS = 4


def sent_to_all(array, axis):
    length = lax.axis_size(axis)
    return lax.all_to_all(
        jnp.broadcast_to(array[None], (length, *array.shape)), axis, 0, 0, tiled=True
    )


def joined_along(blocks, dim):
    blocks = jnp.moveaxis(blocks, 0, dim)
    lengths = blocks.shape
    return blocks.reshape(*lengths[:dim], lengths[dim] * lengths[dim + 1], *lengths[dim + 2 :])


def gather_directly(array, axis, dim):
    blocks = sent_to_all(array, axis)
    return joined_along(blocks, dim)


def gathered_once(array, axis):
    leaves = jax.tree.leaves(array)
    turns = sorted(range(len(leaves)), key=lambda k: -leaves[k].size)
    width = (1, *leaves[turns[0]].shape)[-1]
    lines = [
        jnp.pad(leaves[k].reshape(-1), (0, -leaves[k].size % width)).reshape(-1, width)
        for k in turns
    ]
    both, at, found = (sent_to_all(jnp.concatenate(lines), axis), 0, {})
    for k, line in zip(turns, lines):
        slab = both[:, at : at + len(line)].reshape(len(both), -1)
        found[k] = slab[:, : leaves[k].size].reshape(-1, *leaves[k].shape)
        at += len(line)
    numbers = iter(range(len(leaves)))
    return jax.tree.map(lambda _: found[next(numbers)], array)


def joined_by_halves(pieces, combine):
    while len(jax.tree.leaves(pieces)[0]) > 1:
        pieces = jax.vmap(combine)(
            *(jax.tree.map(lambda part: part[side::2], pieces) for side in (0, 1))
        )
    return jax.tree.map(lambda part: part[0], pieces)


def joined_all(array, axis, combine):
    pieces = gathered_once(array, axis)
    return joined_by_halves(pieces, combine)


def split_up(array, dim, length):
    before, after = (array.shape[:dim], array.shape[dim + 1 :])
    return jnp.moveaxis(array.reshape(*before, length, -1, *after), dim, 0)


def summed_on_arrival(array, axis, dim):
    length = lax.axis_size(axis)
    blocks = lax.all_to_all(split_up(array, dim, length), axis, 0, 0, tiled=True)
    return jnp.sum(blocks, axis=0)


def of_everyone(array, axis):
    everything = sent_to_all(array, axis)
    return jnp.sum(everything, axis=0)


def sum_at_owner(array, axis, dim):
    length = lax.axis_size(axis)
    blocks = lax.all_to_all(split_up(array, dim, length), axis, 0, 0, tiled=True)
    return jnp.sum(blocks.astype(jnp.float32), axis=0)


def local_partials(grouped_queries, keys_per_page, values_per_page, usable):
    local_rows, kv_heads, block_length, head_size = grouped_queries.shape
    scores = jnp.einsum(
        "skgd,slkd->skgl", grouped_queries, keys_per_page, preferred_element_type=jnp.float32
    ) / math.sqrt(head_size)
    scores = jnp.where(usable[:, None, None, :], scores, -1e30)
    maxima = jnp.max(scores, axis=-1)
    powers = jnp.exp(scores - maxima[..., None])
    totals = jnp.sum(powers, axis=-1)
    weights = powers.astype(jnp.bfloat16)
    weighted = jnp.einsum(
        "skgl,slkd->skgd", weights, values_per_page, preferred_element_type=jnp.float32
    )
    heads_all = kv_heads * block_length
    return (
        maxima.reshape(local_rows, heads_all),
        totals.reshape(local_rows, heads_all),
        weighted.reshape(local_rows, heads_all, head_size),
    )


def combine_partials(first, second):
    max_first, sum_first, out_first = first
    max_second, sum_second, out_second = second
    joint_max = jnp.maximum(max_first, max_second)
    scale_first = jnp.exp(max_first - joint_max)
    scale_second = jnp.exp(max_second - joint_max)
    return (
        joint_max,
        sum_first * scale_first + sum_second * scale_second,
        out_first * scale_first[..., None] + out_second * scale_second[..., None],
    )


def slot_table(expert_ids, expert_count, capacity):
    flat_ids = expert_ids.reshape(-1)
    ordinal = jnp.arange(flat_ids.shape[0], dtype=jnp.int32)
    before = (flat_ids[:, None] == flat_ids[None, :]) & (ordinal[None, :] < ordinal[:, None])
    slot_of = jnp.sum(before.astype(jnp.int32), axis=1)
    target = flat_ids * capacity + slot_of
    return jnp.arange(expert_count * capacity, dtype=jnp.int32)[:, None] == target[None, :]


def per_device(
    hidden_state,
    queries,
    page_table,
    lengths,
    paged_keys,
    paged_values,
    out_weight,
    norm_gain,
    expert_ids,
    route_weights,
    expert_gate,
    expert_up,
    expert_down,
):
    seq_count = lax.axis_size("seq")
    expert_count = lax.axis_size("expert")
    batch_count = lax.axis_size("batch")
    seq_index = lax.axis_index("seq")
    local_rows = queries.shape[0]
    block_length = QUERY_HEADS // KEY_VALUE_HEADS
    heads_here = QUERY_HEADS // seq_count
    page_tables = page_table[:, 0, :]
    keys_per_page = paged_keys[0][page_tables].reshape(
        local_rows, SEQUENCE_SLOTS * PAGE_TOKENS, KEY_VALUE_HEADS, HEAD_DIM
    )
    values_per_page = paged_values[0][page_tables].reshape(
        local_rows, SEQUENCE_SLOTS * PAGE_TOKENS, KEY_VALUE_HEADS, HEAD_DIM
    )
    positions = (
        (jnp.arange(SEQUENCE_SLOTS, dtype=jnp.int32)[:, None] * seq_count + seq_index) * PAGE_TOKENS
        + jnp.arange(PAGE_TOKENS, dtype=jnp.int32)[None, :]
    ).reshape(-1)
    usable = positions[None, :] < lengths[:, None]
    every_head = gather_directly(queries, "seq", 1)
    partials = local_partials(
        every_head.reshape(local_rows, KEY_VALUE_HEADS, block_length, HEAD_DIM),
        keys_per_page,
        values_per_page,
        usable,
    )
    merged = joined_all(partials, "seq", combine_partials)
    first_head = seq_index * heads_here
    totals = lax.dynamic_slice_in_dim(merged[1], first_head, heads_here, 1)
    weighted = lax.dynamic_slice_in_dim(merged[2], first_head, heads_here, 1)
    attention = (
        (weighted / totals[..., None])
        .reshape(local_rows, heads_here * HEAD_DIM)
        .astype(jnp.bfloat16)
    )
    every_row = gather_directly(attention, "expert", 0)
    partial_cols = jnp.dot(every_row, out_weight, preferred_element_type=jnp.float32).reshape(
        expert_count, local_rows, -1
    )
    projected = lax.all_to_all(
        partial_cols, "expert", split_axis=0, concat_axis=2, tiled=True
    ).reshape(local_rows, -1)
    projected = summed_on_arrival(projected, "seq", 1)
    resid = hidden_state.astype(jnp.float32) + projected
    squares = of_everyone(jnp.sum(resid * resid, axis=1), "seq")
    normed = (resid * lax.rsqrt(squares / D + 1e-05)[:, None] * norm_gain[None, :]).astype(
        jnp.bfloat16
    )
    capacity = min(local_rows, max(2, 4 * local_rows // expert_count))
    placed = (
        slot_table(expert_ids, expert_count, capacity)
        .reshape(expert_count * capacity, local_rows, 2)
        .astype(jnp.float32)
    )
    dispatch = jnp.sum(placed, axis=2).astype(jnp.bfloat16)
    mixing = jnp.einsum("rsk,sk->sr", placed, route_weights, precision=lax.Precision.HIGHEST)
    whole_tokens = gather_directly(normed, "seq", 1)
    buffer = (
        jnp.dot(dispatch, whole_tokens, preferred_element_type=jnp.float32)
        .astype(jnp.bfloat16)
        .reshape(expert_count, capacity, D)
    )
    received = lax.all_to_all(buffer, "expert", split_axis=0, concat_axis=0, tiled=True)
    slot_count = received.shape[1]
    region = expert_count * slot_count
    stacked = gather_directly(received, "batch", 0)
    token_rows = stacked.reshape(-1, D)
    gate_part = jnp.dot(token_rows, expert_gate[0], preferred_element_type=jnp.float32)
    up_part = jnp.dot(token_rows, expert_up[0], preferred_element_type=jnp.float32)
    activated = (jax.nn.silu(gate_part) * up_part).astype(jnp.bfloat16)
    act_groups = activated.reshape(batch_count, region, -1)
    down_groups = expert_down[0].reshape(expert_down.shape[1], seq_count, D // seq_count)
    partial_out = jnp.einsum(
        "brf,fsd->sbrd", act_groups, down_groups, preferred_element_type=jnp.float32
    )
    partial_out = partial_out.reshape(seq_count * batch_count, region, D // seq_count)
    summed = sum_at_owner(partial_out.astype(jnp.bfloat16), ("seq", "batch"), 0)[0]
    expert_out = lax.all_to_all(
        summed.reshape(expert_count, slot_count, -1),
        "expert",
        split_axis=0,
        concat_axis=0,
        tiled=True,
    )
    expert_mix = jnp.dot(
        mixing,
        expert_out.reshape(expert_count * capacity, -1),
        precision=lax.Precision.HIGHEST,
        preferred_element_type=jnp.float32,
    )
    return (resid + expert_mix).astype(jnp.bfloat16)


def solution(mesh):
    in_specs = (
        P(("batch", "expert"), "seq"),
        P(("batch", "expert"), "seq"),
        P(("batch", "expert"), "seq", None),
        P(("batch", "expert")),
        P(("batch", "expert"), "seq", None, None),
        P(("batch", "expert"), "seq", None, None),
        P("seq", "expert"),
        P("seq"),
        P(("batch", "expert"), None),
        P(("batch", "expert"), None),
        P("expert", None, ("seq", "batch")),
        P("expert", None, ("seq", "batch")),
        P("expert", ("seq", "batch"), None),
    )
    out_specs = P(("batch", "expert"), "seq")
    return jax.shard_map(
        per_device, mesh=mesh, in_specs=in_specs, out_specs=out_specs, check_vma=False
    )
```

profile of v0, /device:TPU:1, one launch (start us, length us, event | category | flops | bytes accessed | tf_op | source)
XLA Modules:
  0.0 170.7 jit_solution(220219705194561677)
XLA Ops:
  1.4 9.2 %all-to-all-start = ((bf16[16,4,128]{2,1,0:T(4,128)(2,1)}), bf16[16,4,128]{2,1,0:T(4,128)(2,1)S(1)}, u32[]{:S(2)}, u32[]{:S(2)}) async-start(bf16[16,4,128]{2,1,0:T(4,128)(2,1)} %broadcast_in_dim.25), calls=%async_computation | async-start | bytes 32768 | tf_op jit(solution)/shard_map/all_to_all | solution.py:18
  14.2 4.0 %reshape.213 = bf16[4,512,4,128]{3,2,1,0:T(4,128)(2,1)} reshape(bf16[16,128,512]{2,1,0:T(8,128)(2,1)} %gather_fusion) | data formatting | bytes 4194304 | tf_op jit(solution)/shard_map/reshape | solution.py:152
  18.2 3.7 %gather_fusion.1 = bf16[16,128,512]{2,1,0:T(8,128)(2,1)} fusion(bf16[20,128,512]{2,1,0:T(8,128)(2,1)} %bitcast.86, s32[1024]{0:T(1024)S(1)} %pad_clamp_fusion), kind=kCustom, calls=%fused_computation.1 | custom fusion | bytes 4194368 | tf_op jit(solution)/shard_map/gather | solution.py:155
  21.9 4.0 %reshape.214 = bf16[4,512,4,128]{3,2,1,0:T(4,128)(2,1)} reshape(bf16[16,128,512]{2,1,0:T(8,128)(2,1)} %gather_fusion.1) | data formatting | bytes 4194304 | tf_op jit(solution)/shard_map/reshape | solution.py:155
  25.9 2.3 %fusion.51 = (f32[4,4,4]{2,1,0:T(4,128)S(1)}, f32[4,4,4,512]{3,2,1,0:T(4,128)S(1)}) fusion(bf16[4,4,4,128]{3,2,1,0:T(4,128)(2,1)S(1)} %bitcast.93, bf16[4,512,4,128]{3,2,1,0:T(4,128)(2,1)} %reshape.213, pred[4,512]{1,0:T(4,128)(4,1)S(1)} %broadcast_compare_fusion), kind=kOutput, calls=%fused_computation.84 | convolution fusion | flops 8486848 | bytes 2246912 | tf_op jit(solution)/shard_map/skgd,slkd->skgl/dot_general | solution.py:88
  31.5 7.1 %all-to-all-start.1 = ((f32[16,66,128]{2,1,0:T(8,128)}), f32[16,66,128]{2,1,0:T(8,128)S(1)}, u32[]{:S(2)}, u32[]{:S(2)}) async-start(f32[16,66,128]{2,1,0:T(8,128)} %broadcast_in_dim.27), calls=%async_computation.1 | async-start | bytes 1179648 | tf_op jit(solution)/shard_map/all_to_all | solution.py:18
  38.6 17.1 %all-to-all-done.1 = f32[16,66,128]{2,1,0:T(8,128)S(1)} async-done(((f32[16,66,128]{2,1,0:T(8,128)}), f32[16,66,128]{2,1,0:T(8,128)S(1)}, u32[]{:S(2)}, u32[]{:S(2)}) %all-to-all-start.1) | async-done | bytes 540704 | tf_op jit(solution)/shard_map/all_to_all | solution.py:18
  57.1 10.4 %all_to_all.66 = bf16[8,4,128]{2,1,0:T(4,128)(2,1)S(1)} all-to-all(bf16[8,4,128]{2,1,0:T(4,128)(2,1)S(1)} %broadcast_in_dim.28), channel_id=1, replica_groups=mesh['seq'=16,'expert'=8,'batch'=2] {'expert'}, dimensions={0} | all-to-all | bytes 16384 | tf_op jit(solution)/shard_map/all_to_all | solution.py:18
  67.6 8.6 %all_to_all.67 = f32[8,4,512]{2,1,0:T(4,128)} all-to-all(f32[8,4,512]{2,1,0:T(4,128)S(1)} %fusion.33), channel_id=1, replica_groups=mesh['seq'=16,'expert'=8,'batch'=2] {'expert'}, dimensions={0} | all-to-all | bytes 131072 | tf_op jit(solution)/shard_map/all_to_all | solution.py:183
  76.2 3.5 %all-to-all-start.4 = ((f32[16,4,256]{2,1,0:T(4,128)}), f32[16,4,256]{2,1,0:T(4,128)S(1)}, u32[]{:S(2)}, u32[]{:S(2)}) async-start(f32[16,4,256]{2,1,0:T(4,128)} %bitcast.20), calls=%async_computation.4 | async-start | bytes 131072 | tf_op jit(solution)/shard_map/all_to_all | solution.py:71
  80.2 6.5 %all-to-all-done.4 = f32[16,4,256]{2,1,0:T(4,128)S(1)} async-done(((f32[16,4,256]{2,1,0:T(4,128)}), f32[16,4,256]{2,1,0:T(4,128)S(1)}, u32[]{:S(2)}, u32[]{:S(2)}) %all-to-all-start.4) | async-done | bytes 65568 | tf_op jit(solution)/shard_map/all_to_all | solution.py:71
  87.4 3.4 %all-to-all-start.5 = ((f32[16,1,4]{2,1,0:T(1,128)}), f32[16,1,4]{2,1,0:T(1,128)S(1)}, u32[]{:S(2)}, u32[]{:S(2)}) async-start(f32[16,1,4]{2,1,0:T(1,128)} %broadcast_in_dim.29), calls=%async_computation.5 | async-start | bytes 16384 | tf_op jit(solution)/shard_map/all_to_all | solution.py:18
  90.9 6.6 %all-to-all-done.5 = f32[16,1,4]{2,1,0:T(1,128)S(1)} async-done(((f32[16,1,4]{2,1,0:T(1,128)}), f32[16,1,4]{2,1,0:T(1,128)S(1)}, u32[]{:S(2)}, u32[]{:S(2)}) %all-to-all-start.5) | async-done | bytes 288 | tf_op jit(solution)/shard_map/all_to_all | solution.py:18
  98.3 3.5 %all-to-all-start.6 = ((bf16[16,4,256]{2,1,0:T(4,128)(2,1)}), bf16[16,4,256]{2,1,0:T(4,128)(2,1)S(1)}, u32[]{:S(2)}, u32[]{:S(2)}) async-start(bf16[16,4,256]{2,1,0:T(4,128)(2,1)} %broadcast_in_dim.30), calls=%async_computation.6 | async-start | bytes 65536 | tf_op jit(solution)/shard_map/all_to_all | solution.py:18
  101.9 6.7 %all-to-all-done.6 = bf16[16,4,256]{2,1,0:T(4,128)(2,1)S(1)} async-done(((bf16[16,4,256]{2,1,0:T(4,128)(2,1)}), bf16[16,4,256]{2,1,0:T(4,128)(2,1)S(1)}, u32[]{:S(2)}, u32[]{:S(2)}) %all-to-all-start.6) | async-done | bytes 32800 | tf_op jit(solution)/shard_map/all_to_all | solution.py:18
  108.9 11.8 %all_to_all.68 = bf16[8,2,4096]{2,1,0:T(2,128)(2,1)S(1)} all-to-all(bf16[8,2,4096]{2,1,0:T(2,128)(2,1)S(1)} %reshape.223), channel_id=1, replica_groups=mesh['seq'=16,'expert'=8,'batch'=2] {'expert'}, dimensions={0} | all-to-all | bytes 262144 | tf_op jit(solution)/shard_map/all_to_all | solution.py:206
  121.7 5.5 %all-to-all-start.8 = ((bf16[2,8,2,4096]{3,2,1,0:T(2,128)(2,1)}), bf16[2,8,2,4096]{3,2,1,0:T(2,128)(2,1)S(1)}, u32[]{:S(2)}, u32[]{:S(2)}) async-start(bf16[2,8,2,4096]{3,2,1,0:T(2,128)(2,1)} %broadcast_in_dim.31), calls=%async_computation.8 | async-start | bytes 524288 | tf_op jit(solution)/shard_map/all_to_all | solution.py:18
  127.2 3.6 %copy.75 = bf16[32,8,16,256]{3,2,1,0:T(8,128)(2,1)} copy(bf16[32,8,16,256]{3,1,2,0:T(8,128)(2,1)} %bitcast.84) | data formatting | bytes 4194304
  130.7 4.5 %all-to-all-done.8 = bf16[2,8,2,4096]{3,2,1,0:T(2,128)(2,1)S(1)} async-done(((bf16[2,8,2,4096]{3,2,1,0:T(2,128)(2,1)}), bf16[2,8,2,4096]{3,2,1,0:T(2,128)(2,1)S(1)}, u32[]{:S(2)}, u32[]{:S(2)}) %all-to-all-start.8) | async-done | bytes 262176 | tf_op jit(solution)/shard_map/all_to_all | solution.py:18
  135.3 2.2 %fusion.4 = f32[32,256]{1,0:T(8,128)S(1)} fusion(bf16[32,4096]{1,0:T(8,128)(2,1)S(1)} %reshape_reshape.24, bf16[1,4096,256]{2,1,0:T(8,128)(2,1)} %param.23), kind=kOutput, calls=%fused_computation.7 | convolution fusion | flops 67108864 | bytes 2392064 | tf_op jit(solution)/shard_map/dot_general | solution.py:211
  141.1 6.3 %all-to-all-start.9 = ((bf16[32,1,16,256]{3,2,1,0:T(8,128)(2,1)}), bf16[32,1,16,256]{3,2,1,0:T(8,128)(2,1)S(1)}, u32[]{:S(2)}, u32[]{:S(2)}) async-start(bf16[32,1,16,256]{3,2,1,0:T(8,128)(2,1)} %bitcast.34), calls=%async_computation.9 | async-start | bytes 524288 | tf_op jit(solution)/shard_map/all_to_all | solution.py:82
  147.6 10.0 %all-to-all-done.9 = bf16[32,1,16,256]{3,2,1,0:T(8,128)(2,1)S(1)} async-done(((bf16[32,1,16,256]{3,2,1,0:T(8,128)(2,1)}), bf16[32,1,16,256]{3,2,1,0:T(8,128)(2,1)S(1)}, u32[]{:S(2)}, u32[]{:S(2)}) %all-to-all-start.9) | async-done | bytes 262176 | tf_op jit(solution)/shard_map/all_to_all | solution.py:82
  158.2 7.1 %all-to-all-start.10 = ((f32[8,2,256]{2,1,0:T(2,128)}), f32[8,2,256]{2,1,0:T(2,128)S(1)}, u32[]{:S(2)}, u32[]{:S(2)}) async-start(f32[8,2,256]{2,1,0:T(2,128)} %reshape_squeeze.7), calls=%async_computation.10 | async-start | bytes 32768 | tf_op jit(solution)/shard_map/all_to_all | solution.py:221
  165.4 4.5 %all-to-all-done.10 = f32[8,2,256]{2,1,0:T(2,128)S(1)} async-done(((f32[8,2,256]{2,1,0:T(2,128)}), f32[8,2,256]{2,1,0:T(2,128)S(1)}, u32[]{:S(2)}, u32[]{:S(2)}) %all-to-all-start.10) | async-done | bytes 16416 | tf_op jit(solution)/shard_map/all_to_all | solution.py:221
  (78 shorter events, 18.4 us)
Async XLA Ops:
  0.0 12.2 %copy-start = (bf16[1,20,128,512]{3,2,1,0:T(8,128)(2,1)S(1)}, bf16[1,20,128,512]{3,2,1,0:T(8,128)(2,1)}, u32[]{:S(2)}) copy-start(bf16[1,20,128,512]{3,2,1,0:T(8,128)(2,1)} %param.17) | copy-start | bytes 7864324
  1.4 24.4 %all-to-all-start = ((bf16[16,4,128]{2,1,0:T(4,128)(2,1)}), bf16[16,4,128]{2,1,0:T(4,128)(2,1)S(1)}, u32[]{:S(2)}, u32[]{:S(2)}) async-start(bf16[16,4,128]{2,1,0:T(4,128)(2,1)} %broadcast_in_dim.25), calls=%async_computation | async-start | bytes 32768 | tf_op jit(solution)/shard_map/all_to_all | solution.py:18
  31.5 35.9 %copy-start.2 = (bf16[128,512]{1,0:T(8,128)(2,1)S(1)}, bf16[128,512]{1,0:T(8,128)(2,1)}, u32[]{:S(2)}) copy-start(bf16[128,512]{1,0:T(8,128)(2,1)} %param.19) | copy-start | bytes 393220
  31.5 48.2 %copy-start.4 = (s32[4,2]{0,1:T(2,128)S(1)}, s32[4,2]{0,1:T(2,128)}, u32[]{:S(2)}) copy-start(s32[4,2]{0,1:T(2,128)} %param.21) | copy-start | bytes 100
  31.5 24.3 %all-to-all-start.1 = ((f32[16,66,128]{2,1,0:T(8,128)}), f32[16,66,128]{2,1,0:T(8,128)S(1)}, u32[]{:S(2)}, u32[]{:S(2)}) async-start(f32[16,66,128]{2,1,0:T(8,128)} %broadcast_in_dim.27), calls=%async_computation.1 | async-start | bytes 1179648 | tf_op jit(solution)/shard_map/all_to_all | solution.py:18
  38.6 48.1 %copy-start.3 = (bf16[4,256]{1,0:T(4,128)(2,1)S(1)}, bf16[4,256]{1,0:T(4,128)(2,1)}, u32[]{:S(2)}) copy-start(bf16[4,256]{1,0:T(4,128)(2,1)} %param.13) | copy-start | bytes 6148
  38.6 59.0 %copy-start.5 = (f32[256]{0:T(256)S(1)}, f32[256]{0:T(256)}, u32[]{:S(2)}) copy-start(f32[256]{0:T(256)} %param.20) | copy-start | bytes 3076
  76.2 10.4 %all-to-all-start.4 = ((f32[16,4,256]{2,1,0:T(4,128)}), f32[16,4,256]{2,1,0:T(4,128)S(1)}, u32[]{:S(2)}, u32[]{:S(2)}) async-start(f32[16,4,256]{2,1,0:T(4,128)} %bitcast.20), calls=%async_computation.4 | async-start | bytes 131072 | tf_op jit(solution)/shard_map/all_to_all | solution.py:71
  87.4 10.1 %all-to-all-start.5 = ((f32[16,1,4]{2,1,0:T(1,128)}), f32[16,1,4]{2,1,0:T(1,128)S(1)}, u32[]{:S(2)}, u32[]{:S(2)}) async-start(f32[16,1,4]{2,1,0:T(1,128)} %broadcast_in_dim.29), calls=%async_computation.5 | async-start | bytes 16384 | tf_op jit(solution)/shard_map/all_to_all | solution.py:18
  98.3 10.3 %all-to-all-start.6 = ((bf16[16,4,256]{2,1,0:T(4,128)(2,1)}), bf16[16,4,256]{2,1,0:T(4,128)(2,1)S(1)}, u32[]{:S(2)}, u32[]{:S(2)}) async-start(bf16[16,4,256]{2,1,0:T(4,128)(2,1)} %broadcast_in_dim.30), calls=%async_computation.6 | async-start | bytes 65536 | tf_op jit(solution)/shard_map/all_to_all | solution.py:18
  121.7 13.5 %all-to-all-start.8 = ((bf16[2,8,2,4096]{3,2,1,0:T(2,128)(2,1)}), bf16[2,8,2,4096]{3,2,1,0:T(2,128)(2,1)S(1)}, u32[]{:S(2)}, u32[]{:S(2)}) async-start(bf16[2,8,2,4096]{3,2,1,0:T(2,128)(2,1)} %broadcast_in_dim.31), calls=%async_computation.8 | async-start | bytes 524288 | tf_op jit(solution)/shard_map/all_to_all | solution.py:18
  135.3 4.3 %copy-start.1 = (bf16[32,8,16,256]{3,2,1,0:T(8,128)(2,1)S(1)}, bf16[32,8,16,256]{3,2,1,0:T(8,128)(2,1)}, u32[]{:S(2)}) copy-start(bf16[32,8,16,256]{3,2,1,0:T(8,128)(2,1)} %copy.75) | copy-start | bytes 6291460
  139.6 7.8 %copy-start.6 = (f32[4,2]{0,1:T(2,128)S(1)}, f32[4,2]{0,1:T(2,128)}, u32[]{:S(2)}) copy-start(f32[4,2]{0,1:T(2,128)} %param.22) | copy-start | bytes 100
  141.1 16.5 %all-to-all-start.9 = ((bf16[32,1,16,256]{3,2,1,0:T(8,128)(2,1)}), bf16[32,1,16,256]{3,2,1,0:T(8,128)(2,1)S(1)}, u32[]{:S(2)}, u32[]{:S(2)}) async-start(bf16[32,1,16,256]{3,2,1,0:T(8,128)(2,1)} %bitcast.34), calls=%async_computation.9 | async-start | bytes 524288 | tf_op jit(solution)/shard_map/all_to_all | solution.py:82
  158.2 11.7 %all-to-all-start.10 = ((f32[8,2,256]{2,1,0:T(2,128)}), f32[8,2,256]{2,1,0:T(2,128)S(1)}, u32[]{:S(2)}, u32[]{:S(2)}) async-start(f32[8,2,256]{2,1,0:T(2,128)} %reshape_squeeze.7), calls=%async_computation.10 | async-start | bytes 32768 | tf_op jit(solution)/shard_map/all_to_all | solution.py:221
where the time goes:
time: 172 us; the launch traced here: 171 us
  waiting for transfers between devices  55.9 us (32%)
  starting transfers between devices  45.5 us (26%)
  blocking collectives  30.8 us (18%)
  local copies, waits for them, and re-layouts  24.5 us (14%)
  matrix products  10.6 us (6%)
  other arithmetic  3.02 us (2%)
    all_to_all x5, waiting for transfers between devices, sent_to_all(): lax.all_to_all(jnp.broadcast_to(array[None], (length, *array.shape)), axi...  34.9 us
    all_to_all x5, starting transfers between devices, sent_to_all(): lax.all_to_all(jnp.broadcast_to(array[None], (length, *array.shape)), axi...  28.6 us
    all_to_all x1, blocking collectives, per_device(): lax.all_to_all(buffer, 'expert', split_axis=0, concat_axis=0, tiled=True)  11.8 us
    all_to_all x1, blocking collectives, sent_to_all(): lax.all_to_all(jnp.broadcast_to(array[None], (length, *array.shape)), axi...  10.4 us
    all_to_all x1, waiting for transfers between devices, sum_at_owner(): lax.all_to_all(split_up(array, dim, length), axis, 0, 0, tiled=True)  9.99 us
    all_to_all x1, blocking collectives, per_device(): lax.all_to_all(partial_cols, 'expert', split_axis=0, concat_axis=2, tiled...  8.6 us
    all_to_all x1, starting transfers between devices, per_device(): lax.all_to_all(summed.reshape(expert_count, slot_count, -1), 'expert', sp...  7.05 us
    all_to_all x1, waiting for transfers between devices, summed_on_arrival(): lax.all_to_all(split_up(array, dim, length), axis, 0, 0, tiled=True)  6.47 us
  transfers between devices with their start and end apart: 8, of which 7 were waited for; matrix products, arithmetic and copies ran while one was open for 12% of the time, Pallas kernels for 0%

commit v1 on v0

v1 whole, which is shorter than its diff:
```python
import functools
import math

import jax
import jax.numpy as jnp
from jax import lax
from jax.experimental import pallas as pl
from jax.experimental.pallas import tpu as pltpu
from jax.sharding import PartitionSpec as P

D = 4096
QUERY_HEADS = 16
KEY_VALUE_HEADS = 4
HEAD_DIM = 128
PAGE_TOKENS = 128
SLOTS = 4
ROWS = 4
SEQ = 16
EXPERTS = 8
BATCHES = 2
POOL = 20
FEATURES = D // SEQ
HIDDEN = 256
QUARTER = D // 4
BF = jnp.bfloat16
F32 = jnp.float32
MESH = pl.DeviceIdType.MESH


def iota(shape, dim):
    return lax.broadcasted_iota(jnp.int32, shape, dim)


def kernel(
    hidden_ref, query_ref, table_ref, length_ref, keys_hbm, values_hbm, weight_hbm, gain_ref,
    ids_ref, route_ref, gate_hbm, up_hbm, down_hbm, out_ref,
    keys, values, gate, up, down, weights,
    query_buf, query_rows, part, part_buf, proj, proj_buf, info, slabs, tokens,
    sent, slots, returned, results, terms, term_buf,
    local_sems, send_sems, recv_sems,
):
    s = lax.axis_index("seq")
    e = lax.axis_index("expert")
    b = lax.axis_index("batch")
    me = b * SEQ + s

    local = [
        pltpu.make_async_copy(source, target, local_sems.at[k])
        for k, (source, target) in enumerate((
            (keys_hbm, keys), (values_hbm, values), (weight_hbm, weights.at[e]),
            (gate_hbm, gate), (up_hbm, up), (down_hbm, down),
        ))
    ]
    for copy in local:
        copy.start()

    def seq_peer(d):
        return lax.rem(s + d, SEQ)

    def expert_peer(d):
        return lax.rem(e + d, EXPERTS)

    def pair_peer(d):
        return lax.rem(me + d, BATCHES * SEQ)

    barrier = pltpu.get_barrier_semaphore()
    for d in range(1, SEQ):
        pl.semaphore_signal(barrier, 1, device_id={"seq": seq_peer(d)}, device_id_type=MESH)
    for d in range(1, EXPERTS):
        pl.semaphore_signal(barrier, 1, device_id={"expert": expert_peer(d)}, device_id_type=MESH)
    pl.semaphore_signal(barrier, 1, device_id={"batch": 1 - b}, device_id_type=MESH)

    ids = [[ids_ref[t, k] for k in range(2)] for t in range(ROWS)]
    row8, lane8 = iota((8, 128), 0), iota((8, 128), 1)
    slab = jnp.full((8, 128), -1.0, F32)
    for t in range(ROWS):
        for k in range(2):
            earlier = jnp.int32(0)
            for a in range(2 * t + k):
                earlier = earlier + jnp.where(ids[a // 2][a % 2] == ids[t][k], 1, 0)
            target = (ids[t][k] * 2 + earlier).astype(F32)
            slab = jnp.where((row8 == t) & (lane8 == k), target, slab)
            slab = jnp.where((row8 == t) & (lane8 == 2 + k), route_ref[t, k], slab)
    info[b] = slab
    tokens[...] = jnp.zeros_like(tokens)
    query_buf[s] = query_ref[...]

    pl.semaphore_wait(barrier, SEQ - 1 + EXPERTS - 1 + 1)

    def send(source, target, phase, device):
        pltpu.make_async_remote_copy(
            src_ref=source, dst_ref=target, send_sem=send_sems.at[phase],
            recv_sem=recv_sems.at[phase], device_id=device, device_id_type=MESH,
        ).start()

    def whole(ref, phase):
        return pltpu.make_async_remote_copy(
            src_ref=ref, dst_ref=ref, send_sem=send_sems.at[phase],
            recv_sem=recv_sems.at[phase], device_id={"batch": 1 - b}, device_id_type=MESH,
        )

    for d in range(1, SEQ):
        send(query_ref, query_buf.at[s], 0, {"seq": seq_peer(d)})
    send(info.at[b], info.at[b], 1, {"batch": 1 - b})
    for d in range(1, EXPERTS):
        send(weight_hbm, weights.at[e], 2, {"expert": expert_peer(d)})

    local[0].wait()
    local[1].wait()
    whole(query_buf.at[pl.ds(0, SEQ - 1)], 0).wait_recv()
    for h in range(QUERY_HEADS):
        query_rows[pl.ds(ROWS * h, ROWS), :] = query_buf[h].astype(F32)
    width = KEY_VALUE_HEADS * HEAD_DIM
    own_group = iota((QUERY_HEADS, width), 1) // HEAD_DIM == iota((QUERY_HEADS, width), 0) // 4
    spot = iota((QUERY_HEADS, SLOTS * PAGE_TOKENS), 1)
    position = (spot // PAGE_TOKENS * SEQ + s) * PAGE_TOKENS + spot % PAGE_TOKENS
    group_of = iota((QUERY_HEADS, HEAD_DIM), 0) // 4
    lane16 = iota((QUERY_HEADS, HEAD_DIM), 1)
    for i in range(ROWS):
        q = query_rows[pl.ds(i, QUERY_HEADS, stride=ROWS), :]
        q = jnp.where(own_group, jnp.concatenate([q] * KEY_VALUE_HEADS, axis=1), 0.0).astype(BF)
        pages = [table_ref[i, j] for j in range(SLOTS)]
        k = jnp.concatenate([keys[page] for page in pages], axis=0)
        scores = lax.dot_general(
            q, k, (((1,), (1,)), ((), ())), preferred_element_type=F32
        ) * (1.0 / math.sqrt(HEAD_DIM))
        scores = jnp.where(position < length_ref[i], scores, -1e30)
        peak = jnp.max(scores, axis=1, keepdims=True)
        powers = jnp.exp(scores - peak)
        total = jnp.sum(powers, axis=1, keepdims=True)
        v = jnp.concatenate([values[page] for page in pages], axis=0)
        mixed = jnp.dot(powers.astype(BF), v, preferred_element_type=F32)
        picked = jnp.zeros((QUERY_HEADS, HEAD_DIM), F32)
        for g in range(KEY_VALUE_HEADS):
            picked = jnp.where(group_of == g, mixed[:, g * HEAD_DIM : (g + 1) * HEAD_DIM], picked)
        part[pl.ds(i, QUERY_HEADS, stride=8), :] = picked
        part[pl.ds(ROWS + i, QUERY_HEADS, stride=8), :] = jnp.where(lane16 < 64, peak, total)

    def head_part(h):
        return part.at[pl.ds(pl.multiple_of(h * 8, 8), 8)]

    for d in range(1, SEQ):
        send(head_part(seq_peer(d)), part_buf.at[s], 3, {"seq": seq_peer(d)})
    part_buf[s] = part[pl.ds(pl.multiple_of(s * 8, 8), 8), :]
    whole(part_buf.at[pl.ds(0, SEQ - 1)], 3).wait_recv()
    lower = lane8 < 64
    joint = part_buf[0]
    for h in range(1, SEQ):
        joint = jnp.maximum(joint, part_buf[h])
    above = jnp.zeros((8, 128), F32)
    below = jnp.zeros((8, 128), F32)
    for h in range(SEQ):
        piece = part_buf[h]
        factor = jnp.exp(jnp.where((row8 >= ROWS) & lower, piece - joint, 0.0))
        factor = jnp.where(lower, factor, pltpu.roll(factor, 64, 1))
        below = below + factor * piece
        above = above + pltpu.roll(factor, ROWS, 0) * piece
    below = jnp.where(lower, pltpu.roll(below, 64, 1), below)
    below = pltpu.roll(below, ROWS, 0)
    attention = jnp.where(row8 < ROWS, above / jnp.where(row8 < ROWS, below, 1.0), 0.0).astype(BF)

    local[2].wait()
    whole(weights.at[pl.ds(0, EXPERTS - 1)], 2).wait_recv()
    for k in range(EXPERTS):
        columns = jnp.dot(attention, weights[k], preferred_element_type=F32)
        for side in range(2):
            proj[2 * k + side] = columns[:ROWS, side * FEATURES : (side + 1) * FEATURES]
    for d in range(1, SEQ):
        send(proj.at[seq_peer(d)], proj_buf.at[s], 4, {"seq": seq_peer(d)})
    proj_buf[s] = proj[s]
    whole(proj_buf.at[pl.ds(0, SEQ - 1)], 4).wait_recv()
    resid = proj_buf[0]
    for h in range(1, SEQ):
        resid = resid + proj_buf[h]
    resid = hidden_ref[...].astype(F32) + resid

    square = jnp.sum(resid * resid, axis=1, keepdims=True)
    high = square.astype(BF).astype(F32)
    tail = jnp.where(iota((ROWS, 128), 1) < 64, high, square - high)
    slabs[me, :, pl.ds(0, FEATURES)] = (resid * gain_ref[...]).astype(BF)
    slabs[me, :, pl.ds(FEATURES, 128)] = tail.astype(BF)
    for d in range(1, BATCHES * SEQ):
        peer = pair_peer(d)
        send(slabs.at[me], slabs.at[me], 5, {"batch": peer // SEQ, "seq": lax.rem(peer, SEQ)})
    whole(slabs.at[pl.ds(0, BATCHES * SEQ - 1)], 5).wait_recv()
    for block in range(BATCHES):
        squares = jnp.zeros((ROWS, 128), F32)
        for n in range(SEQ):
            squares = squares + slabs[block * SEQ + n, :, pl.ds(FEATURES, 128)].astype(F32)
        squares = squares + pltpu.roll(squares, 64, 1)
        scale = lax.rsqrt(squares / D + 1e-05)
        scale = jnp.concatenate([scale, scale], axis=1)
        for n in range(SEQ):
            row, column = ((n // 4) * BATCHES + block) * 8, (n % 4) * FEATURES
            tokens[pl.ds(row, ROWS), pl.ds(column, FEATURES)] = (
                slabs[block * SEQ + n, :, pl.ds(0, FEATURES)].astype(F32) * scale
            )

    whole(info.at[0], 1).wait_recv()
    facts = jnp.concatenate([info[0], info[1]] * 4, axis=0)
    row64, lane64 = iota((64, 128), 0), iota((64, 128), 1)
    same = (row64 // 16 == lane64 // 4 % 4) & (row64 // 8 % 2 == lane64 // 2 % 2)
    slot = (lane64 // 16 * 2 + lane64 % 2).astype(F32)
    hits = [same & (facts[:, k : k + 1] == slot) for k in range(2)]
    placing = jnp.where(hits[0] | hits[1], 1.0, 0.0).astype(BF)
    mixing = jnp.where(hits[0], facts[:, 2:3], 0.0) + jnp.where(hits[1], facts[:, 3:4], 0.0)
    placed = lax.dot_general(
        placing, tokens[...].astype(BF), (((0,), (0,)), ((), ())), preferred_element_type=F32
    ).astype(BF)
    for k in range(EXPERTS):
        sent[k] = placed[16 * k : 16 * (k + 1), :]
    for d in range(1, EXPERTS):
        send(sent.at[expert_peer(d)], slots.at[e], 6, {"expert": expert_peer(d)})
    slots[e] = sent[e]
    for copy in local[3:]:
        copy.wait()
    whole(slots.at[pl.ds(0, EXPERTS - 1)], 6).wait_recv()

    rows = slots[...].reshape(128, QUARTER)
    quarter_of = iota((128, QUARTER), 0) // 4 % 4
    gate_sum = jnp.zeros((128, HIDDEN), F32)
    up_sum = jnp.zeros((128, HIDDEN), F32)
    for n in range(4):
        mine = jnp.where(quarter_of == n, rows, jnp.zeros_like(rows))
        gate_sum += jnp.dot(mine, gate[pl.ds(n * QUARTER, QUARTER), :], preferred_element_type=F32)
        up_sum += jnp.dot(mine, up[pl.ds(n * QUARTER, QUARTER), :], preferred_element_type=F32)

    def folded(array):
        array = array.reshape(EXPERTS, 16, HIDDEN)
        array = array[:, :8] + array[:, 8:]
        return (array + pltpu.roll(array, 4, 1)).reshape(EXPERTS * 8, HIDDEN)

    gate_part, up_part = folded(gate_sum), folded(up_sum)
    act = (gate_part / (1.0 + jnp.exp(-gate_part)) * up_part).astype(BF)
    first = iota((64, QUARTER), 0) % 8 < 4
    halves = []
    for n in range(0, 4, 2):
        pair = [
            jnp.dot(act, down[:, pl.ds((n + m) * QUARTER, QUARTER)], preferred_element_type=F32)
            for m in range(2)
        ]
        halves.append(jnp.where(first, pair[0], pair[1]))
    for k in range(EXPERTS):
        returned[k] = jnp.concatenate(
            [half[8 * k : 8 * (k + 1)] for half in halves], axis=0
        ).astype(BF)
    for d in range(1, EXPERTS):
        send(returned.at[expert_peer(d)], results.at[e], 7, {"expert": expert_peer(d)})
    results[e] = returned[e]
    whole(results.at[pl.ds(0, EXPERTS - 1)], 7).wait_recv()

    found = results[...].reshape(128, QUARTER)
    rest = mixing
    merged = jnp.zeros((64, QUARTER), F32)
    for _ in range(3):
        top = rest.astype(BF)
        rest = rest - top.astype(F32)
        merged += jnp.dot(top, found, preferred_element_type=F32)
    for block in range(BATCHES):
        for n in range(SEQ):
            row, column = ((n // 4) * BATCHES + block) * 8, (n % 4) * FEATURES
            terms[block * SEQ + n] = merged[row : row + ROWS, column : column + FEATURES].astype(BF)
    for d in range(1, BATCHES * SEQ):
        peer = pair_peer(d)
        send(terms.at[peer], term_buf.at[me], 8, {"batch": peer // SEQ, "seq": lax.rem(peer, SEQ)})
    term_buf[me] = terms[me]
    whole(term_buf.at[pl.ds(0, BATCHES * SEQ - 1)], 8).wait_recv()
    expert_sum = jnp.zeros((ROWS, FEATURES), F32)
    for n in range(BATCHES * SEQ):
        expert_sum = expert_sum + term_buf[n].astype(F32)
    out_ref[...] = (resid + expert_sum).astype(BF)

    for phase, ref in enumerate((
        query_buf.at[pl.ds(0, SEQ - 1)], info.at[0], weights.at[pl.ds(0, EXPERTS - 1)],
        part_buf.at[pl.ds(0, SEQ - 1)], proj_buf.at[pl.ds(0, SEQ - 1)],
        slabs.at[pl.ds(0, BATCHES * SEQ - 1)], slots.at[pl.ds(0, EXPERTS - 1)],
        results.at[pl.ds(0, EXPERTS - 1)], term_buf.at[pl.ds(0, BATCHES * SEQ - 1)],
    )):
        whole(ref, phase).wait_send()


def per_device(
    hidden_state, queries, page_table, lengths, paged_keys, paged_values, out_weight, norm_gain,
    expert_ids, route_weights, expert_gate, expert_up, expert_down,
):
    vmem = pl.BlockSpec(memory_space=pltpu.VMEM)
    smem = pl.BlockSpec(memory_space=pltpu.SMEM)
    hbm = pl.BlockSpec(memory_space=pl.ANY)
    return pl.pallas_call(
        kernel,
        out_shape=jax.ShapeDtypeStruct((ROWS, FEATURES), BF),
        in_specs=[vmem, vmem, smem, smem, hbm, hbm, hbm, vmem, smem, smem, hbm, hbm, hbm],
        out_specs=vmem,
        scratch_shapes=[
            pltpu.VMEM((POOL, PAGE_TOKENS, 512), BF),
            pltpu.VMEM((POOL, PAGE_TOKENS, 512), BF),
            pltpu.VMEM((D, HIDDEN), BF),
            pltpu.VMEM((D, HIDDEN), BF),
            pltpu.VMEM((HIDDEN, D), BF),
            pltpu.VMEM((EXPERTS, HEAD_DIM, 512), BF),
            pltpu.VMEM((SEQ, ROWS, HEAD_DIM), BF),
            pltpu.VMEM((SEQ * ROWS, HEAD_DIM), F32),
            pltpu.VMEM((SEQ * 8, HEAD_DIM), F32),
            pltpu.VMEM((SEQ, 8, HEAD_DIM), F32),
            pltpu.VMEM((SEQ, ROWS, FEATURES), F32),
            pltpu.VMEM((SEQ, ROWS, FEATURES), F32),
            pltpu.VMEM((BATCHES, 8, 128), F32),
            pltpu.VMEM((BATCHES * SEQ, ROWS, FEATURES + 128), BF),
            pltpu.VMEM((64, QUARTER), F32),
            pltpu.VMEM((EXPERTS, 16, QUARTER), BF),
            pltpu.VMEM((EXPERTS, 16, QUARTER), BF),
            pltpu.VMEM((EXPERTS, 16, QUARTER), BF),
            pltpu.VMEM((EXPERTS, 16, QUARTER), BF),
            pltpu.VMEM((BATCHES * SEQ, ROWS, FEATURES), BF),
            pltpu.VMEM((BATCHES * SEQ, ROWS, FEATURES), BF),
            pltpu.SemaphoreType.DMA((6,)),
            pltpu.SemaphoreType.DMA((9,)),
            pltpu.SemaphoreType.DMA((9,)),
        ],
        compiler_params=pltpu.CompilerParams(collective_id=0, has_side_effects=True),
        name="layer",
    )(
        hidden_state, queries, page_table[:, 0], lengths, paged_keys[0], paged_values[0],
        out_weight, norm_gain[None], expert_ids, route_weights, expert_gate[0], expert_up[0],
        expert_down[0],
    )


def solution(mesh):
    rows = P(("batch", "expert"), "seq")
    pages = P(("batch", "expert"), "seq", None, None)
    in_specs = (
        rows, rows, P(("batch", "expert"), "seq", None), P(("batch", "expert")), pages, pages,
        P("seq", "expert"), P("seq"), P(("batch", "expert"), None), P(("batch", "expert"), None),
        P("expert", None, ("seq", "batch")), P("expert", None, ("seq", "batch")),
        P("expert", ("seq", "batch"), None),
    )
    return jax.shard_map(
        per_device, mesh=mesh, in_specs=in_specs, out_specs=rows, check_vma=False
    )
```

time: 172 us -> 58.4 us (0.34)
  waiting for transfers between devices: 55.9 us -> 0 us
  Pallas kernels: 0 us -> 54.2 us
  starting transfers between devices: 45.5 us -> 0 us
  blocking collectives: 30.8 us -> 0 us
  local copies, waits for them, and re-layouts: 24.5 us -> 3.94 us
  matrix products: 10.6 us -> 0 us
  other arithmetic: 3.02 us -> 0 us
    all_to_all x8 -> x0, waiting for transfers between devices: 55.9 us -> none  [the longest x5 34.9 us: sent_to_all(): lax.all_to_all(jnp.broadcast_to(array[None], (length, *array.shape)), axi...]
    pallas_call x0 -> x1, Pallas kernels: none -> 54.2 us  [per_device(): pl.pallas_call(kernel, out_shape=jax.ShapeDtypeStruct((ROWS, FEATURES), B...]
    all_to_all x8 -> x0, starting transfers between devices: 45.5 us -> none  [the longest x5 28.6 us: sent_to_all(): lax.all_to_all(jnp.broadcast_to(array[None], (length, *array.shape)), axi...]
    all_to_all x3 -> x0, blocking collectives: 30.8 us -> none  [the longest x1 11.8 us: per_device(): lax.all_to_all(buffer, 'expert', split_axis=0, concat_axis=0, tiled=True)]
    dot_general x9 -> x0, matrix products: 10.6 us -> none  [the longest x1 2.33 us: local_partials(): jnp.einsum('skgd,slkd->skgl', grouped_queries, keys_per_page, preferred_e...]
    reshape x7 -> x0, local copies, waits for them, and re-layouts: 8.19 us -> none  [the longest x1 3.95 us: per_device(): paged_values[0][page_tables]]
    gather x2 -> x0, local copies, waits for them, and re-layouts: 5.73 us -> none  [the longest x1 3.74 us: per_device(): paged_values[0][page_tables]]
    broadcast_in_dim x6 -> x0, local copies, waits for them, and re-layouts: 4.45 us -> none  [sent_to_all(): jnp.broadcast_to(array[None], (length, *array.shape))]
  transfers between devices with their start and end apart: 8 -> 0, of which waited for: 7 -> 0; matrix products, arithmetic and copies ran while one was open for 12% -> 0% of each run, Pallas kernels for 0% -> 0%
where the time goes in v1:
time: 58.4 us; the launch traced here: 58.2 us
  Pallas kernels  54.2 us (93%)
  local copies, waits for them, and re-layouts  3.94 us (7%)
    pallas_call x1, Pallas kernels, per_device(): pl.pallas_call(kernel, out_shape=jax.ShapeDtypeStruct((ROWS, FEATURES), B...  54.2 us
    unnamed x3, local copies, waits for them, and re-layouts  3.94 us

profile of v1, /device:TPU:1, one launch (start us, length us, event | category | flops | bytes accessed | tf_op | source)
XLA Modules:
  0.0 58.2 jit_solution(5819441317806184763)
XLA Ops:
  0.0 1.3 %copy.14.ids_ref = s32[4,2]{1,0:T(4,128)} copy(s32[4,2]{0,1:T(2,128)} %param.21) | data formatting | bytes 64 | tf_op args[8]
  1.3 1.4 %copy.15.route_ref = f32[4,2]{1,0:T(4,128)} copy(f32[4,2]{0,1:T(2,128)} %param.22) | data formatting | bytes 64 | tf_op args[9]
  2.7 54.2 %layer.1 = bf16[4,256]{1,0:T(4,128)(2,1)} custom-call(bf16[4,256]{1,0:T(4,128)(2,1)} %hidden_ref.1, bf16[4,128]{1,0:T(4,128)(2,1)} %query_ref.1, s32[4,4]{1,0:T(4,128)} %bitcast.12, s32[4]{0:T(128)} %length_ref.1, bf16[20,128,512]{2,1,0:T(8,128)(2,1)} %bitcast.7, bf16[20,128,512]{2,1,0:T(8,128)(2,1)} %bitcast.8, bf16[128,512]{1,0:T(8,128)(2,1)} %weight_hbm.1, ...), custom_call_target="tpu_custom_call" | custom-call | tf_op jit(solution)/shard_map/layer/pallas_call | solution.py:289
  56.9 1.3 %copy.17 = bf16[4,256]{1,0:T(4,128)(2,1)} copy(bf16[4,256]{1,0:T(4,128)(2,1)} %layer.1) | data formatting | bytes 4096

commit v2 on v1

v2 whole, which is shorter than its diff:
```python
import functools
import math

import jax
import jax.numpy as jnp
from jax import lax
from jax.experimental import pallas as pl
from jax.experimental.pallas import tpu as pltpu
from jax.sharding import PartitionSpec as P

D = 4096
QUERY_HEADS = 16
KEY_VALUE_HEADS = 4
HEAD_DIM = 128
PAGE_TOKENS = 128
SLOTS = 4
ROWS = 4
SEQ = 16
EXPERTS = 8
BATCHES = 2
POOL = 20
FEATURES = D // SEQ
HIDDEN = 256
QUARTER = D // 4
BF = jnp.bfloat16
F32 = jnp.float32
MESH = pl.DeviceIdType.MESH


def iota(shape, dim):
    return lax.broadcasted_iota(jnp.int32, shape, dim)


def kernel(
    hidden_hbm, query_hbm, table_hbm, length_hbm, keys_hbm, values_hbm, weight_hbm, gain_hbm,
    ids_hbm, route_hbm, gate_hbm, up_hbm, down_hbm, out_ref,
    hidden_ref, query_ref, gain_ref, table_ref, length_ref, ids_ref, route_ref,
    keys, values, gate, up, down, weights,
    query_buf, query_rows, part, part_buf, proj, proj_buf, info, gains, slabs, tokens, scales,
    sent, slots, scale_sent, scale_buf, scale_rows, frames, returned, results, terms, term_buf,
    local_sems, send_sems, recv_sems,
):
    s = lax.axis_index("seq")
    e = lax.axis_index("expert")
    b = lax.axis_index("batch")
    me = b * SEQ + s

    local = [
        pltpu.make_async_copy(source, target, local_sems.at[k])
        for k, (source, target) in enumerate((
            (query_hbm, query_ref), (ids_hbm, ids_ref), (route_hbm, route_ref),
            (gain_hbm, gain_ref), (weight_hbm, weights.at[e]), (table_hbm, table_ref),
            (length_hbm, length_ref), (keys_hbm, keys), (values_hbm, values),
            (hidden_hbm, hidden_ref), (gate_hbm, gate), (up_hbm, up),
            *((down_hbm.at[:, pl.ds(n * QUARTER, QUARTER)], down.at[n]) for n in range(4)),
        ))
    ]
    for copy in local:
        copy.start()

    def seq_peer(d):
        return lax.rem(s + d, SEQ)

    def expert_peer(d):
        return lax.rem(e + d, EXPERTS)

    def pair_peer(d):
        return lax.rem(me + d, BATCHES * SEQ)

    barrier = pltpu.get_barrier_semaphore()
    for d in range(1, SEQ):
        pl.semaphore_signal(barrier, 1, device_id={"seq": seq_peer(d)}, device_id_type=MESH)
    for d in range(1, EXPERTS):
        pl.semaphore_signal(barrier, 1, device_id={"expert": expert_peer(d)}, device_id_type=MESH)
    pl.semaphore_signal(barrier, 1, device_id={"batch": 1 - b}, device_id_type=MESH)

    for copy in local[:5]:
        copy.wait()

    ids = [[ids_ref[k, t] for k in range(2)] for t in range(ROWS)]
    row8, lane8 = iota((8, 128), 0), iota((8, 128), 1)
    slab = jnp.full((8, 128), -1.0, F32)
    for t in range(ROWS):
        for k in range(2):
            earlier = jnp.int32(0)
            for a in range(2 * t + k):
                earlier = earlier + jnp.where(ids[a // 2][a % 2] == ids[t][k], 1, 0)
            target = (ids[t][k] * 2 + earlier).astype(F32)
            slab = jnp.where((row8 == t) & (lane8 == k), target, slab)
            slab = jnp.where((row8 == t) & (lane8 == 2 + k), route_ref[k, t], slab)
    info[b] = slab
    tokens[...] = jnp.zeros_like(tokens)
    scales[...] = jnp.zeros_like(scales)
    query_buf[s] = query_ref[...]
    gains[s] = gain_ref[...]

    pl.semaphore_wait(barrier, SEQ - 1 + EXPERTS - 1 + 1)

    def send(source, target, phase, device, arrival=None):
        pltpu.make_async_remote_copy(
            src_ref=source, dst_ref=target, send_sem=send_sems.at[phase],
            recv_sem=recv_sems.at[phase if arrival is None else arrival],
            device_id=device, device_id_type=MESH,
        ).start()

    def whole(ref, phase, arrival=None):
        return pltpu.make_async_remote_copy(
            src_ref=ref, dst_ref=ref, send_sem=send_sems.at[phase],
            recv_sem=recv_sems.at[phase if arrival is None else arrival],
            device_id={"batch": 1 - b}, device_id_type=MESH,
        )

    for d in range(1, SEQ):
        send(query_ref, query_buf.at[s], 0, {"seq": seq_peer(d)})
    send(info.at[b], info.at[b], 1, {"batch": 1 - b})
    for d in range(1, SEQ):
        send(gain_ref, gains.at[s], 21, {"seq": seq_peer(d)})
    partner = e + 1 - 2 * lax.rem(e, 2)
    ahead, behind, across = expert_peer(2), expert_peer(6), expert_peer(4)
    send(weights.at[e], weights.at[e], 19, {"expert": ahead})
    send(weights.at[e], weights.at[e], 19, {"expert": behind})
    send(weights.at[e], weights.at[e], 2, {"expert": partner})

    for copy in local[5:9]:
        copy.wait()
    whole(query_buf.at[pl.ds(0, SEQ - 1)], 0).wait_recv()
    half = HEAD_DIM // 2
    whole(weights.at[pl.ds(0, 2)], 19).wait_recv()
    for source, target, start in ((behind, ahead, 0), (ahead, behind, half)):
        piece = weights.at[source, pl.ds(start, half)]
        send(piece, piece, 20, {"expert": target})
    for source in (behind, ahead):
        send(weights.at[source], weights.at[source], 2, {"expert": partner})
    for h in range(QUERY_HEADS):
        query_rows[pl.ds(ROWS * h, ROWS), :] = query_buf[h].astype(F32)
    width = KEY_VALUE_HEADS * HEAD_DIM
    own_group = iota((QUERY_HEADS, width), 1) // HEAD_DIM == iota((QUERY_HEADS, width), 0) // 4
    spot = iota((QUERY_HEADS, SLOTS * PAGE_TOKENS), 1)
    position = (spot // PAGE_TOKENS * SEQ + s) * PAGE_TOKENS + spot % PAGE_TOKENS
    group_of = iota((QUERY_HEADS, HEAD_DIM), 0) // 4
    lane16 = iota((QUERY_HEADS, HEAD_DIM), 1)
    for i in range(ROWS):
        q = query_rows[pl.ds(i, QUERY_HEADS, stride=ROWS), :]
        q = jnp.where(own_group, jnp.concatenate([q] * KEY_VALUE_HEADS, axis=1), 0.0).astype(BF)
        pages = [table_ref[i, j] for j in range(SLOTS)]
        k = jnp.concatenate([keys[page] for page in pages], axis=0)
        scores = lax.dot_general(
            q, k, (((1,), (1,)), ((), ())), preferred_element_type=F32
        ) * (1.0 / math.sqrt(HEAD_DIM))
        scores = jnp.where(position < length_ref[i], scores, -1e30)
        peak = jnp.max(scores, axis=1, keepdims=True)
        powers = jnp.exp(scores - peak)
        total = jnp.sum(powers, axis=1, keepdims=True)
        v = jnp.concatenate([values[page] for page in pages], axis=0)
        mixed = jnp.dot(powers.astype(BF), v, preferred_element_type=F32)
        picked = jnp.zeros((QUERY_HEADS, HEAD_DIM), F32)
        for g in range(KEY_VALUE_HEADS):
            picked = jnp.where(group_of == g, mixed[:, g * HEAD_DIM : (g + 1) * HEAD_DIM], picked)
        part[pl.ds(i, QUERY_HEADS, stride=8), :] = picked
        part[pl.ds(ROWS + i, QUERY_HEADS, stride=8), :] = jnp.where(lane16 < 64, peak, total)

    def head_part(h):
        return part.at[pl.ds(pl.multiple_of(h * 8, 8), 8)]

    for d in range(1, SEQ):
        send(head_part(seq_peer(d)), part_buf.at[s], 3, {"seq": seq_peer(d)})
    part_buf[s] = part[pl.ds(pl.multiple_of(s * 8, 8), 8), :]
    whole(weights.at[0], 20).wait_recv()
    send(weights.at[across], weights.at[across], 2, {"expert": partner})
    whole(part_buf.at[pl.ds(0, SEQ - 1)], 3).wait_recv()
    lower = lane8 < 64
    joint = part_buf[0]
    for h in range(1, SEQ):
        joint = jnp.maximum(joint, part_buf[h])
    above = jnp.zeros((8, 128), F32)
    below = jnp.zeros((8, 128), F32)
    for h in range(SEQ):
        piece = part_buf[h]
        factor = jnp.exp(jnp.where((row8 >= ROWS) & lower, piece - joint, 0.0))
        factor = jnp.where(lower, factor, pltpu.roll(factor, 64, 1))
        below = below + factor * piece
        above = above + pltpu.roll(factor, ROWS, 0) * piece
    below = jnp.where(lower, pltpu.roll(below, 64, 1), below)
    below = pltpu.roll(below, ROWS, 0)
    attention = jnp.where(row8 < ROWS, above / jnp.where(row8 < ROWS, below, 1.0), 0.0).astype(BF)

    whole(weights.at[pl.ds(0, 4)], 2).wait_recv()
    for copy in local[9:10]:
        copy.wait()
    for k in range(EXPERTS):
        columns = jnp.dot(attention, weights[k], preferred_element_type=F32)
        for side in range(2):
            proj[2 * k + side] = columns[:ROWS, side * FEATURES : (side + 1) * FEATURES]
    for d in range(1, SEQ):
        send(proj.at[seq_peer(d)], proj_buf.at[s], 4, {"seq": seq_peer(d)})
    proj_buf[s] = proj[s]
    whole(proj_buf.at[pl.ds(0, SEQ - 1)], 4).wait_recv()
    resid = proj_buf[0]
    for h in range(1, SEQ):
        resid = resid + proj_buf[h]
    resid = hidden_ref[...].astype(F32) + resid

    y, depth = s // 4, b * 4 + lax.rem(s, 4)

    def quarter(d):
        return lax.rem(y + d, 4)

    def column_peer(dy, dz):
        far = lax.rem(depth + dz, 8)
        return quarter(dy), far, {"batch": far // 4, "seq": quarter(dy) * 4 + lax.rem(far, 4)}

    slabs[me] = resid.astype(BF)
    for dy in (2, 1, 3, 0):
        for dz in (4, 3, 5, 2, 6, 1, 7, 0):
            if dy or dz:
                device = column_peer(dy, dz)[2]
                send(slabs.at[me], slabs.at[me], 5, device, 5 + y)
    whole(info.at[0], 1).wait_recv()
    whole(gains.at[pl.ds(0, SEQ - 1)], 21).wait_recv()
    facts = jnp.concatenate([info[0], info[1]], axis=0)
    row16, lane = iota((16, 128), 0), iota((16, 128), 1)

    def hits(stride):
        slot = (lane // stride * 2 + lane % 2).astype(F32)
        same = (row16 // 8 == lane // 2 % 2) & (lane % stride < 4)
        return [same & (facts[:, k : k + 1] == slot) for k in range(2)]

    placed, found = hits(8), hits(4)
    placing = jnp.where(placed[0] | placed[1], 1.0, 0.0).astype(BF)[:, :64]
    rest = jnp.where(found[0], facts[:, 2:3], 0.0) + jnp.where(found[1], facts[:, 3:4], 0.0)

    def three_parts(array):
        parts = []
        for _ in range(3):
            parts.append(array.astype(BF))
            array = array - parts[-1].astype(F32)
        return parts

    mixing = jnp.concatenate(three_parts(rest), axis=0)[:, :32]
    forth, back = (0, 1, 3, 2), (2, 1, 3, 0)
    squares = [jnp.zeros((ROWS, FEATURES), F32) for _ in range(BATCHES)]
    for k, d in enumerate(forth):
        count = 8 if d else 7
        whole(slabs.at[pl.ds(0, count)], 5, 5 + quarter(d)).wait_recv()
        for block in range(BATCHES):
            for n in range(4):
                source = quarter(d) * 4 + n
                piece = slabs[block * SEQ + source].astype(F32)
                squares[block] = squares[block] + piece * piece
                tokens[k, pl.ds(block * 8, ROWS), pl.ds(n * FEATURES, FEATURES)] = (
                    piece * gains[source]
                )
        rows = lax.dot_general(
            placing, tokens[k].astype(BF), (((0,), (0,)), ((), ())), preferred_element_type=F32
        )
        for n in range(EXPERTS):
            sent[k, n] = rows[8 * n : 8 * n + ROWS].astype(BF)
        for n in range(1, EXPERTS):
            peer = expert_peer(n)
            send(sent.at[k, peer], slots.at[k, e], 9, {"expert": peer}, 9 + k)
        slots[k, e] = sent[k, e]
    for block in range(BATCHES):
        mean = jnp.sum(squares[block], axis=1, keepdims=True) / D
        scales[pl.ds(block * 8, ROWS), :] = jnp.broadcast_to(
            lax.rsqrt(mean + 1e-05), (ROWS, 128)
        )
    rows = jnp.zeros((64, 128), F32)
    for piece in three_parts(scales[...]):
        rows += lax.dot_general(
            placing, piece, (((0,), (0,)), ((), ())), preferred_element_type=F32
        )
    for n in range(EXPERTS):
        scale_sent[n] = rows[8 * n : 8 * n + ROWS]
    for n in range(1, EXPERTS):
        peer = expert_peer(n)
        send(scale_sent.at[peer], scale_buf.at[e], 13, {"expert": peer})
    scale_buf[e] = scale_sent[e]

    for copy in local[10:]:
        copy.wait()
    gate_sum = jnp.zeros((32, HIDDEN), F32)
    up_sum = jnp.zeros((32, HIDDEN), F32)
    for k, d in enumerate(forth):
        whole(slots.at[k, pl.ds(0, EXPERTS - 1)], 9, 9 + k).wait_recv()
        for n in range(EXPERTS):
            frames[k, pl.ds(n * ROWS, ROWS), :] = slots[k, n].astype(F32)
        rows = frames[k].astype(BF)
        window = pl.ds(pl.multiple_of(quarter(d) * QUARTER, QUARTER), QUARTER)
        gate_sum += jnp.dot(rows, gate[window, :], preferred_element_type=F32)
        up_sum += jnp.dot(rows, up[window, :], preferred_element_type=F32)
    whole(scale_buf.at[pl.ds(0, EXPERTS - 1)], 13).wait_recv()
    for n in range(EXPERTS):
        scale_rows[pl.ds(n * ROWS, ROWS), :] = scale_buf[n]
    scale = jnp.concatenate([scale_rows[...]] * 2, axis=1)
    gate_part, up_part = gate_sum * scale, up_sum * scale
    act = (gate_part / (1.0 + jnp.exp(-gate_part)) * up_part).astype(BF)
    for k, d in enumerate(back):
        rows = jnp.dot(act, down[quarter(d)], preferred_element_type=F32)
        for n in range(EXPERTS):
            returned[k, n] = rows[ROWS * n : ROWS * (n + 1)].astype(BF)
        for n in range(1, EXPERTS):
            peer = expert_peer(n)
            send(returned.at[k, peer], results.at[k, e], 14, {"expert": peer}, 14 + k)
        results[k, e] = returned[k, e]
    for k, d in enumerate(back):
        whole(results.at[k, pl.ds(0, EXPERTS - 1)], 14, 14 + k).wait_recv()
        for n in range(EXPERTS):
            frames[k, pl.ds(n * ROWS, ROWS), :] = results[k, n].astype(F32)
        rows = jnp.dot(mixing, frames[k].astype(BF), preferred_element_type=F32)
        rows = rows[:16] + rows[16:32] + rows[32:]
        for n in range(8):
            terms[k, n] = rows[
                n // 4 * 8 : n // 4 * 8 + ROWS, n % 4 * FEATURES : (n % 4 + 1) * FEATURES
            ].astype(BF)
        for dz in (4, 3, 5, 2, 6, 1, 7, 0):
            if d or dz:
                _, far, device = column_peer(d, dz)
                send(terms.at[k, far], term_buf.at[me], 18, device)
    term_buf[me] = terms[3, depth]
    whole(term_buf.at[pl.ds(0, BATCHES * SEQ - 1)], 18).wait_recv()
    expert_sum = jnp.zeros((ROWS, FEATURES), F32)
    for n in range(BATCHES * SEQ):
        expert_sum = expert_sum + term_buf[n].astype(F32)
    out_ref[...] = resid + expert_sum

    for phase, ref in (
        (0, query_buf.at[pl.ds(0, SEQ - 1)]), (1, info.at[0]), (2, weights.at[pl.ds(0, 4)]),
        (3, part_buf.at[pl.ds(0, SEQ - 1)]), (4, proj_buf.at[pl.ds(0, SEQ - 1)]),
        (5, slabs.at[pl.ds(0, BATCHES * SEQ - 1)]), (9, slots.at[:, pl.ds(0, EXPERTS - 1)]),
        (13, scale_buf.at[pl.ds(0, EXPERTS - 1)]), (14, results.at[:, pl.ds(0, EXPERTS - 1)]),
        (18, term_buf.at[pl.ds(0, BATCHES * SEQ - 1)]), (19, weights.at[pl.ds(0, 2)]),
        (20, weights.at[0]), (21, gains.at[pl.ds(0, SEQ - 1)]),
    ):
        whole(ref, phase).wait_send()


def per_device(
    hidden_state, queries, page_table, lengths, paged_keys, paged_values, out_weight, norm_gain,
    expert_ids, route_weights, expert_gate, expert_up, expert_down,
):
    hbm = pl.BlockSpec(memory_space=pltpu.HBM)
    result = pl.pallas_call(
        kernel,
        out_shape=jax.ShapeDtypeStruct((ROWS, FEATURES), F32),
        in_specs=[hbm] * 13,
        out_specs=pl.BlockSpec(memory_space=pltpu.VMEM),
        scratch_shapes=[
            pltpu.VMEM((ROWS, FEATURES), BF),
            pltpu.VMEM((ROWS, HEAD_DIM), BF),
            pltpu.VMEM((1, FEATURES), F32),
            pltpu.SMEM((ROWS, SLOTS), jnp.int32),
            pltpu.SMEM((ROWS,), jnp.int32),
            pltpu.SMEM((2, ROWS), jnp.int32),
            pltpu.SMEM((2, ROWS), F32),
            pltpu.VMEM((POOL, PAGE_TOKENS, 512), BF),
            pltpu.VMEM((POOL, PAGE_TOKENS, 512), BF),
            pltpu.VMEM((D, HIDDEN), BF),
            pltpu.VMEM((D, HIDDEN), BF),
            pltpu.VMEM((4, HIDDEN, QUARTER), BF),
            pltpu.VMEM((EXPERTS, HEAD_DIM, 512), BF),
            pltpu.VMEM((SEQ, ROWS, HEAD_DIM), BF),
            pltpu.VMEM((SEQ * ROWS, HEAD_DIM), F32),
            pltpu.VMEM((SEQ * 8, HEAD_DIM), F32),
            pltpu.VMEM((SEQ, 8, HEAD_DIM), F32),
            pltpu.VMEM((SEQ, ROWS, FEATURES), F32),
            pltpu.VMEM((SEQ, ROWS, FEATURES), F32),
            pltpu.VMEM((BATCHES, 8, 128), F32),
            pltpu.VMEM((SEQ, 1, FEATURES), F32),
            pltpu.VMEM((BATCHES * SEQ, ROWS, FEATURES), BF),
            pltpu.VMEM((4, 16, QUARTER), F32),
            pltpu.VMEM((16, 128), F32),
            pltpu.VMEM((4, EXPERTS, ROWS, QUARTER), BF),
            pltpu.VMEM((4, EXPERTS, ROWS, QUARTER), BF),
            pltpu.VMEM((EXPERTS, ROWS, 128), F32),
            pltpu.VMEM((EXPERTS, ROWS, 128), F32),
            pltpu.VMEM((32, 128), F32),
            pltpu.VMEM((4, 32, QUARTER), F32),
            pltpu.VMEM((4, EXPERTS, ROWS, QUARTER), BF),
            pltpu.VMEM((4, EXPERTS, ROWS, QUARTER), BF),
            pltpu.VMEM((4, 8, ROWS, FEATURES), BF),
            pltpu.VMEM((BATCHES * SEQ, ROWS, FEATURES), BF),
            pltpu.SemaphoreType.DMA((16,)),
            pltpu.SemaphoreType.DMA((22,)),
            pltpu.SemaphoreType.DMA((22,)),
        ],
        compiler_params=pltpu.CompilerParams(collective_id=0, has_side_effects=True),
        name="layer",
    )(
        hidden_state, queries, page_table[:, 0], lengths, paged_keys[0], paged_values[0],
        out_weight, norm_gain[None], expert_ids.T, route_weights.T, expert_gate[0], expert_up[0],
        expert_down[0],
    )
    return result.astype(BF)


def solution(mesh):
    rows = P(("batch", "expert"), "seq")
    pages = P(("batch", "expert"), "seq", None, None)
    in_specs = (
        rows, rows, P(("batch", "expert"), "seq", None), P(("batch", "expert")), pages, pages,
        P("seq", "expert"), P("seq"), P(("batch", "expert"), None), P(("batch", "expert"), None),
        P("expert", None, ("seq", "batch")), P("expert", None, ("seq", "batch")),
        P("expert", ("seq", "batch"), None),
    )
    return jax.shard_map(
        per_device, mesh=mesh, in_specs=in_specs, out_specs=rows, check_vma=False
    )
```

time: 58.4 us -> 50.7 us (0.87)
  Pallas kernels: 54.2 us -> 49.3 us
  local copies, waits for them, and re-layouts: 3.94 us -> 0 us
  other arithmetic: 0 us -> 1.26 us
    pallas_call x1, Pallas kernels: 54.2 us -> 49.3 us  [per_device(): pl.pallas_call(kernel, out_shape=jax.ShapeDtypeStruct((ROWS, FEATURES), F...]
    unnamed x3 -> x0, local copies, waits for them, and re-layouts: 3.94 us -> none
    convert_element_type x0 -> x1, other arithmetic: none -> 1.26 us  [per_device(): return result.astype(BF)]
where the time goes in v2:
time: 50.7 us; the launch traced here: 50.6 us
  Pallas kernels  49.3 us (97%)
  other arithmetic  1.26 us (2%)
    pallas_call x1, Pallas kernels, per_device(): pl.pallas_call(kernel, out_shape=jax.ShapeDtypeStruct((ROWS, FEATURES), F...  49.3 us
    convert_element_type x1, other arithmetic, per_device(): return result.astype(BF)  1.26 us

profile of v2, /device:TPU:1, one launch (start us, length us, event | category | flops | bytes accessed | tf_op | source)
XLA Modules:
  0.0 50.6 jit_solution(15625711774758323670)
XLA Ops:
  0.0 49.3 %layer.1 = f32[4,256]{1,0:T(4,128)} custom-call(bf16[4,256]{1,0:T(4,128)(2,1)} %hidden_hbm.1, bf16[4,128]{1,0:T(4,128)(2,1)} %query_hbm.1, s32[4,4]{1,0:T(4,128)} %bitcast.14, s32[4]{0:T(128)} %length_hbm.1, bf16[20,128,512]{2,1,0:T(8,128)(2,1)} %bitcast.9, bf16[20,128,512]{2,1,0:T(8,128)(2,1)} %bitcast.10, bf16[128,512]{1,0:T(8,128)(2,1)} %weight_hbm.1, ...), custom_call_target="tpu_custom_call" | custom-call | tf_op jit(solution)/shard_map/layer/pallas_call | solution.py:342
  49.4 1.3 %convert_element_type.3 = bf16[4,256]{1,0:T(4,128)(2,1)} convert(f32[4,256]{1,0:T(4,128)} %layer.1) | non-fusion elementwise | flops 1024 | bytes 6144 | tf_op jit(solution)/shard_map/convert_element_type | solution.py:393
